TPU v7x, 32 devices: a whole 2x2x4 slice. The times are simulated.
32 devices in a mesh: depth: 32 (over z, y, x, core).
Axes of the slice: x: 2, y: 2, z: 4, core: 2. Of those that a mesh axis runs over, the one named last changes fastest.
Arguments:
- weights: bfloat16 [32, 1024, 1024], P('depth'), may hold values from -0.1875 to 0.1875
- gains: float32 [32, 1024], P('depth'), may hold values from 0.1 to 1.9
- states: float32 [32, 512, 1024], P('depth'), may hold values from -1200 to 1200
- adjoints: float32 [32, 512, 1024], P('depth'), may hold values from -0.26516503 to 0.26516503
Outputs:
- grad_weight: bfloat16 [32, 1024, 1024], P('depth')
- grad_gain: float32 [32, 1024], P('depth')
All inputs are finite; a program needn't handle non-finite values.
Results may differ from a plain program's by a relative error of at most 0.006.
Values sent between devices are 32-bit elements; how exact they have to be, the bound alone decides.
No kernel may reach another device: no remote copies, remote signals or barrier semaphores. Data moves between devices by JAX's collectives and lax.ppermute only.
A program may use at most 64 MiB of HBM per device.

v0:
```python
import jax
import jax.numpy as jnp
from jax import lax
from jax.sharding import PartitionSpec as P

SWEEPS = 4


eps = 1e-06


def passed_along(block, axis, distance):
    devices = range(lax.axis_size(axis))
    route = [(i - distance, i) for i in devices if i - distance in devices]
    return lax.ppermute(block, axis, route)


def layer_terms(state, adjoint, gain_vec, weight):
    inverse = lax.rsqrt(jnp.mean(state * state, axis=-1, keepdims=True) + eps)
    normed = state * inverse
    scaled = (normed * gain_vec[None, :]).astype(jnp.bfloat16)
    preact = jnp.dot(scaled, weight, preferred_element_type=jnp.float32)
    squash = jax.nn.sigmoid(preact)
    output = state + preact * squash
    pre_grad = (adjoint * squash * (1.0 + preact * (1.0 - squash))).astype(jnp.bfloat16)
    feat_grad = lax.dot_general(
        pre_grad, weight, (((1,), (1,)), ((), ())), preferred_element_type=jnp.float32
    )
    gained = feat_grad * gain_vec[None, :]
    carried = adjoint + inverse * (
        gained - normed * jnp.mean(gained * normed, axis=-1, keepdims=True)
    )
    return (output, carried, scaled, pre_grad, normed, feat_grad)


def on_device(weights, gains, states, adjoints):
    weight = weights[0]
    gain_vec = gains[0]
    state = states[0]
    adjoint = adjoints[0]
    count = lax.axis_size("depth")
    index = lax.axis_index("depth")
    is_first = index == 0
    is_last = index == count - 1
    for sweep_index in range(SWEEPS):
        half_rows = state.shape[0] // 2
        upper_parts = []
        lower_parts = []
        for block_index in range(2):
            start_row = block_index * half_rows
            output, carried, scaled, pre_grad, normed, feat_grad = layer_terms(
                state[start_row : start_row + half_rows],
                adjoint[start_row : start_row + half_rows],
                gain_vec,
                weight,
            )
            upper_parts.append(passed_along(output, "depth", 1))
            lower_parts.append(passed_along(carried, "depth", -1))
        arrived_state = jnp.concatenate(upper_parts, axis=0)
        arrived_adjoint = jnp.concatenate(lower_parts, axis=0)
        state = jnp.where(is_first, state, arrived_state)
        adjoint = jnp.where(is_last, adjoint, arrived_adjoint)
    output, carried, scaled, pre_grad, normed, feat_grad = layer_terms(
        state, adjoint, gain_vec, weight
    )
    grad_weight = lax.dot_general(
        scaled, pre_grad, (((0,), (0,)), ((), ())), preferred_element_type=jnp.float32
    )
    grad_gain = jnp.sum(normed * feat_grad, axis=0)
    return (grad_weight.astype(jnp.bfloat16)[None], grad_gain[None])


def solution(mesh):
    placed = (
        P("depth", None, None),
        P("depth", None),
        P("depth", None, None),
        P("depth", None, None),
    )
    return jax.shard_map(
        on_device,
        mesh=mesh,
        in_specs=placed,
        out_specs=(P("depth", None, None), P("depth", None)),
        check_vma=False,
    )
```

profile of v0, /device:TPU:1, one launch (start us, length us, event | category | flops | bytes accessed | tf_op | source)
XLA Modules:
  0.0 238.0 jit_solution(4986276381172618257)
XLA Ops:
  0.7 1.9 fusion.79
  7.9 2.7 %bitcast_add_fusion.1 = (f32[256,1024]{1,0:T(8,128)}, f32[256,1024]{1,0:T(8,128)}, f32[256,1024]{1,0:T(8,128)}, f32[256,1024]{1,0:T(8,128)}) fusion(f32[256,1024]{1,0:T(8,128)S(1)} %get-tuple-element.36, f32[1,512,1024]{2,1,0:T(8,128)S(1)} %copy-done.3, f32[1,512,1024]{2,1,0:T(8,128)S(1)} %copy-done.1, f32[256]{0:T(256)S(1)} %broadcast_multiply_fusion.7, ...), kind=kLoop, calls=%fused_computation.71 | loop fusion | flops 5242880 | bytes 12587008 | tf_op jit(solution)/shard_map/add | solution.py:30
  10.6 4.5 %collective-permute-start = (f32[256,1024]{1,0:T(8,128)}, f32[256,1024]{1,0:T(8,128)S(1)}, u32[]{:S(2)}, u32[]{:S(2)}) collective-permute-start(f32[256,1024]{1,0:T(8,128)} %get-tuple-element.34), channel_id=1, source_target_pairs={{0,1},{1,2},{2,3},{3,4},{4,5},{5,6},{6,7},{7,8},{8,9},{9,10},{10,1... | collective-permute-start | bytes 3145736 | tf_op jit(solution)/shard_map/ppermute | solution.py:15
  15.1 1.9 collective-permute-start.1
  17.0 3.4 %collective-permute-start.8 = (f32[256,1024]{1,0:T(8,128)}, f32[256,1024]{1,0:T(8,128)}, u32[]{:S(2)}, u32[]{:S(2)}) collective-permute-start(f32[256,1024]{1,0:T(8,128)} %get-tuple-element.26), channel_id=1, source_target_pairs={{1,0},{2,1},{3,2},{4,3},{5,4},{6,5},{7,6},{8,7},{9,8},{10,9},{11,1... | collective-permute-start | bytes 3145736 | tf_op jit(solution)/shard_map/ppermute | solution.py:15
  20.4 1.9 collective-permute-start.9
  22.3 27.3 %collective-permute-done = f32[256,1024]{1,0:T(8,128)S(1)} collective-permute-done((f32[256,1024]{1,0:T(8,128)}, f32[256,1024]{1,0:T(8,128)S(1)}, u32[]{:S(2)}, u32[]{:S(2)}) %collective-permute-start) | collective-permute-done | bytes 1048608 | tf_op jit(solution)/shard_map/ppermute | solution.py:15
  49.6 11.2 %collective-permute-done.1 = f32[256,1024]{1,0:T(8,128)} collective-permute-done((f32[256,1024]{1,0:T(8,128)}, f32[256,1024]{1,0:T(8,128)}, u32[]{:S(2)}, u32[]{:S(2)}) %collective-permute-start.1) | collective-permute-done | bytes 1048608 | tf_op jit(solution)/shard_map/ppermute | solution.py:15
  60.8 2.4 %maximum_select_fusion = f32[512,1024]{1,0:T(8,128)S(1)} fusion(f32[256,1024]{1,0:T(8,128)} %collective-permute-done.1, f32[256,1024]{1,0:T(8,128)S(1)} %collective-permute-done, f32[1,512,1024]{2,1,0:T(8,128)} %param.6, pred[]{:T(512)S(6)} %eq.6), kind=kLoop, calls=%fused_computation | loop fusion | flops 1048576 | bytes 6291457 | tf_op jit(solution)/shard_map/jit(_where)/select_n | solution.py:61
  65.8 2.0 maximum_select_fusion.4
  70.1 4.4 %collective-permute-start.2 = (f32[256,1024]{1,0:T(8,128)S(1)}, f32[256,1024]{1,0:T(8,128)S(1)}, u32[]{:S(2)}, u32[]{:S(2)}) collective-permute-start(f32[256,1024]{1,0:T(8,128)S(1)} %get-tuple-element.32), channel_id=1, source_target_pairs={{0,1},{1,2},{2,3},{3,4},{4,5},{5,6},{6,7},{7,8},{8,9},{9,10},{10,1... | collective-permute-start | bytes 3145736 | tf_op jit(solution)/shard_map/ppermute | solution.py:15
  74.5 1.9 collective-permute-start.3
  76.9 2.5 %collective-permute-start.10 = (f32[256,1024]{1,0:T(8,128)S(1)}, f32[256,1024]{1,0:T(8,128)S(1)}, u32[]{:S(2)}, u32[]{:S(2)}) collective-permute-start(f32[256,1024]{1,0:T(8,128)S(1)} %get-tuple-element.24), channel_id=1, source_target_pairs={{1,0},{2,1},{3,2},{4,3},{5,4},{6,5},{7,6},{8,7},{9,8},{10,9},{11,1... | collective-permute-start | bytes 3145736 | tf_op jit(solution)/shard_map/ppermute | solution.py:15
  79.4 2.1 collective-permute-start.11
  81.5 27.2 %collective-permute-done.2 = f32[256,1024]{1,0:T(8,128)S(1)} collective-permute-done((f32[256,1024]{1,0:T(8,128)S(1)}, f32[256,1024]{1,0:T(8,128)S(1)}, u32[]{:S(2)}, u32[]{:S(2)}) %collective-permute-start.2) | collective-permute-done | bytes 1048608 | tf_op jit(solution)/shard_map/ppermute | solution.py:15
  108.7 11.2 %collective-permute-done.3 = f32[256,1024]{1,0:T(8,128)S(1)} collective-permute-done((f32[256,1024]{1,0:T(8,128)S(1)}, f32[256,1024]{1,0:T(8,128)S(1)}, u32[]{:S(2)}, u32[]{:S(2)}) %collective-permute-start.3) | collective-permute-done | bytes 1048608 | tf_op jit(solution)/shard_map/ppermute | solution.py:15
  124.8 4.4 %collective-permute-start.4 = (f32[256,1024]{1,0:T(8,128)S(1)}, f32[256,1024]{1,0:T(8,128)S(1)}, u32[]{:S(2)}, u32[]{:S(2)}) collective-permute-start(f32[256,1024]{1,0:T(8,128)S(1)} %get-tuple-element.30), channel_id=1, source_target_pairs={{0,1},{1,2},{2,3},{3,4},{4,5},{5,6},{6,7},{7,8},{8,9},{9,10},{10,1... | collective-permute-start | bytes 3145736 | tf_op jit(solution)/shard_map/ppermute | solution.py:15
  129.2 1.9 collective-permute-start.5
  131.6 2.5 %collective-permute-start.12 = (f32[256,1024]{1,0:T(8,128)S(1)}, f32[256,1024]{1,0:T(8,128)S(1)}, u32[]{:S(2)}, u32[]{:S(2)}) collective-permute-start(f32[256,1024]{1,0:T(8,128)S(1)} %get-tuple-element.22), channel_id=1, source_target_pairs={{1,0},{2,1},{3,2},{4,3},{5,4},{6,5},{7,6},{8,7},{9,8},{10,9},{11,1... | collective-permute-start | bytes 3145736 | tf_op jit(solution)/shard_map/ppermute | solution.py:15
  134.1 1.9 collective-permute-start.13
  136.0 27.4 %collective-permute-done.4 = f32[256,1024]{1,0:T(8,128)S(1)} collective-permute-done((f32[256,1024]{1,0:T(8,128)S(1)}, f32[256,1024]{1,0:T(8,128)S(1)}, u32[]{:S(2)}, u32[]{:S(2)}) %collective-permute-start.4) | collective-permute-done | bytes 1048608 | tf_op jit(solution)/shard_map/ppermute | solution.py:15
  163.4 11.2 %collective-permute-done.5 = f32[256,1024]{1,0:T(8,128)S(1)} collective-permute-done((f32[256,1024]{1,0:T(8,128)S(1)}, f32[256,1024]{1,0:T(8,128)S(1)}, u32[]{:S(2)}, u32[]{:S(2)}) %collective-permute-start.5) | collective-permute-done | bytes 1048608 | tf_op jit(solution)/shard_map/ppermute | solution.py:15
  178.1 1.5 multiply_reduce_fusion.3
  179.6 4.4 %collective-permute-start.6 = (f32[256,1024]{1,0:T(8,128)S(1)}, f32[256,1024]{1,0:T(8,128)S(1)}, u32[]{:S(2)}, u32[]{:S(2)}) collective-permute-start(f32[256,1024]{1,0:T(8,128)S(1)} %get-tuple-element.28), channel_id=1, source_target_pairs={{0,1},{1,2},{2,3},{3,4},{4,5},{5,6},{6,7},{7,8},{8,9},{9,10},{10,1... | collective-permute-start | bytes 3145736 | tf_op jit(solution)/shard_map/ppermute | solution.py:15
  184.0 1.9 collective-permute-start.7
  186.5 2.5 %collective-permute-start.14 = (f32[256,1024]{1,0:T(8,128)S(1)}, f32[256,1024]{1,0:T(8,128)S(1)}, u32[]{:S(2)}, u32[]{:S(2)}) collective-permute-start(f32[256,1024]{1,0:T(8,128)S(1)} %get-tuple-element.20), channel_id=1, source_target_pairs={{1,0},{2,1},{3,2},{4,3},{5,4},{6,5},{7,6},{8,7},{9,8},{10,9},{11,1... | collective-permute-start | bytes 3145736 | tf_op jit(solution)/shard_map/ppermute | solution.py:15
  189.0 2.3 collective-permute-start.15
  191.2 27.0 %collective-permute-done.6 = f32[256,1024]{1,0:T(8,128)S(1)} collective-permute-done((f32[256,1024]{1,0:T(8,128)S(1)}, f32[256,1024]{1,0:T(8,128)S(1)}, u32[]{:S(2)}, u32[]{:S(2)}) %collective-permute-start.6) | collective-permute-done | bytes 1048608 | tf_op jit(solution)/shard_map/ppermute | solution.py:15
  218.2 11.2 %collective-permute-done.7 = f32[256,1024]{1,0:T(8,128)S(1)} collective-permute-done((f32[256,1024]{1,0:T(8,128)S(1)}, f32[256,1024]{1,0:T(8,128)S(1)}, u32[]{:S(2)}, u32[]{:S(2)}) %collective-permute-start.7) | collective-permute-done | bytes 1048608 | tf_op jit(solution)/shard_map/ppermute | solution.py:15
  229.9 3.6 %fusion.2 = bf16[512,1024]{1,0:T(8,128)(2,1)S(1)} fusion(f32[512,1024]{1,0:T(8,128)S(1)} %maximum_select_fusion.6, f32[256,1024]{1,0:T(8,128)S(1)} %collective-permute-done.15, f32[256,1024]{1,0:T(8,128)S(1)} %collective-permute-done.14, bf16[1,1024,1024]{2,1,0:T(8,128)(2,1)S(1)} %copy-done, f32[1,512,1024]{2,1,0:T(8,128)S(1)} %copy-done.2, ...), kind=kOutput, calls=%fused_computation.10 | convolution fusion | flops 1085276160 | bytes 17831938 | tf_op jit(solution)/shard_map/dot_general | solution.py:22
  233.4 1.9 multiply_reduce_fusion
  235.3 2.7 %convert_bitcast_fusion = bf16[1,1024,1024]{2,1,0:T(8,128)(2,1)} fusion(bf16[512,1024]{1,0:T(8,128)(2,1)S(1)} %fusion.2, f32[512,1024]{1,0:T(8,128)S(1)} %get-tuple-element.19, f32[1024]{0:T(1024)S(1)} %bitcast.147, f32[512]{0:T(512)S(1)} %add_rsqrt_fusion), kind=kOutput, calls=%fused_computation.55 | convolution fusion | flops 1076363264 | bytes 5249024 | tf_op jit(solution)/shard_map/dot_general | solution.py:66
  (62 shorter events, 20.1 us)
Async XLA Ops:
  0.6 2.2 copy-start
  0.6 2.8 %copy-start.1 = (f32[1,512,1024]{2,1,0:T(8,128)S(1)}, f32[1,512,1024]{2,1,0:T(8,128)}, u32[]{:S(2)}) copy-start(f32[1,512,1024]{2,1,0:T(8,128)} %param.6) | copy-start | bytes 6291460
  0.7 2.8 %copy-start.5 = (f32[1,1024]{1,0:T(1,128)S(1)}, f32[1,1024]{1,0:T(1,128)}, u32[]{:S(2)}) copy-start(f32[1,1024]{1,0:T(1,128)} %param.5) | copy-start | bytes 12292
  4.3 1.6 copy-start.3
  10.6 39.0 %collective-permute-start = (f32[256,1024]{1,0:T(8,128)}, f32[256,1024]{1,0:T(8,128)S(1)}, u32[]{:S(2)}, u32[]{:S(2)}) collective-permute-start(f32[256,1024]{1,0:T(8,128)} %get-tuple-element.34), channel_id=1, source_target_pairs={{0,1},{1,2},{2,3},{3,4},{4,5},{5,6},{6,7},{7,8},{8,9},{9,10},{10,1... | collective-permute-start | bytes 3145736 | tf_op jit(solution)/shard_map/ppermute | solution.py:15
  15.1 45.7 %collective-permute-start.1 = (f32[256,1024]{1,0:T(8,128)}, f32[256,1024]{1,0:T(8,128)}, u32[]{:S(2)}, u32[]{:S(2)}) collective-permute-start(f32[256,1024]{1,0:T(8,128)} %get-tuple-element.35), channel_id=1, source_target_pairs={{0,1},{1,2},{2,3},{3,4},{4,5},{5,6},{6,7},{7,8},{8,9},{9,10},{10,1... | collective-permute-start | bytes 3145736 | tf_op jit(solution)/shard_map/ppermute | solution.py:15
  17.0 48.0 %collective-permute-start.8 = (f32[256,1024]{1,0:T(8,128)}, f32[256,1024]{1,0:T(8,128)}, u32[]{:S(2)}, u32[]{:S(2)}) collective-permute-start(f32[256,1024]{1,0:T(8,128)} %get-tuple-element.26), channel_id=1, source_target_pairs={{1,0},{2,1},{3,2},{4,3},{5,4},{6,5},{7,6},{8,7},{9,8},{10,9},{11,1... | collective-permute-start | bytes 3145736 | tf_op jit(solution)/shard_map/ppermute | solution.py:15
  20.4 44.7 %collective-permute-start.9 = (f32[256,1024]{1,0:T(8,128)}, f32[256,1024]{1,0:T(8,128)}, u32[]{:S(2)}, u32[]{:S(2)}) collective-permute-start(f32[256,1024]{1,0:T(8,128)} %get-tuple-element.27), channel_id=1, source_target_pairs={{1,0},{2,1},{3,2},{4,3},{5,4},{6,5},{7,6},{8,7},{9,8},{10,9},{11,1... | collective-permute-start | bytes 3145736 | tf_op jit(solution)/shard_map/ppermute | solution.py:15
  64.3 1.6 copy-start.4
  70.1 38.6 %collective-permute-start.2 = (f32[256,1024]{1,0:T(8,128)S(1)}, f32[256,1024]{1,0:T(8,128)S(1)}, u32[]{:S(2)}, u32[]{:S(2)}) collective-permute-start(f32[256,1024]{1,0:T(8,128)S(1)} %get-tuple-element.32), channel_id=1, source_target_pairs={{0,1},{1,2},{2,3},{3,4},{4,5},{5,6},{6,7},{7,8},{8,9},{9,10},{10,1... | collective-permute-start | bytes 3145736 | tf_op jit(solution)/shard_map/ppermute | solution.py:15
  74.5 45.4 %collective-permute-start.3 = (f32[256,1024]{1,0:T(8,128)S(1)}, f32[256,1024]{1,0:T(8,128)S(1)}, u32[]{:S(2)}, u32[]{:S(2)}) collective-permute-start(f32[256,1024]{1,0:T(8,128)S(1)} %get-tuple-element.33), channel_id=1, source_target_pairs={{0,1},{1,2},{2,3},{3,4},{4,5},{5,6},{6,7},{7,8},{8,9},{9,10},{10,1... | collective-permute-start | bytes 3145736 | tf_op jit(solution)/shard_map/ppermute | solution.py:15
  76.9 45.2 %collective-permute-start.10 = (f32[256,1024]{1,0:T(8,128)S(1)}, f32[256,1024]{1,0:T(8,128)S(1)}, u32[]{:S(2)}, u32[]{:S(2)}) collective-permute-start(f32[256,1024]{1,0:T(8,128)S(1)} %get-tuple-element.24), channel_id=1, source_target_pairs={{1,0},{2,1},{3,2},{4,3},{5,4},{6,5},{7,6},{8,7},{9,8},{10,9},{11,1... | collective-permute-start | bytes 3145736 | tf_op jit(solution)/shard_map/ppermute | solution.py:15
  79.4 42.7 %collective-permute-start.11 = (f32[256,1024]{1,0:T(8,128)S(1)}, f32[256,1024]{1,0:T(8,128)S(1)}, u32[]{:S(2)}, u32[]{:S(2)}) collective-permute-start(f32[256,1024]{1,0:T(8,128)S(1)} %get-tuple-element.25), channel_id=1, source_target_pairs={{1,0},{2,1},{3,2},{4,3},{5,4},{6,5},{7,6},{8,7},{9,8},{10,9},{11,1... | collective-permute-start | bytes 3145736 | tf_op jit(solution)/shard_map/ppermute | solution.py:15
  124.8 38.6 %collective-permute-start.4 = (f32[256,1024]{1,0:T(8,128)S(1)}, f32[256,1024]{1,0:T(8,128)S(1)}, u32[]{:S(2)}, u32[]{:S(2)}) collective-permute-start(f32[256,1024]{1,0:T(8,128)S(1)} %get-tuple-element.30), channel_id=1, source_target_pairs={{0,1},{1,2},{2,3},{3,4},{4,5},{5,6},{6,7},{7,8},{8,9},{9,10},{10,1... | collective-permute-start | bytes 3145736 | tf_op jit(solution)/shard_map/ppermute | solution.py:15
  129.2 45.4 %collective-permute-start.5 = (f32[256,1024]{1,0:T(8,128)S(1)}, f32[256,1024]{1,0:T(8,128)S(1)}, u32[]{:S(2)}, u32[]{:S(2)}) collective-permute-start(f32[256,1024]{1,0:T(8,128)S(1)} %get-tuple-element.31), channel_id=1, source_target_pairs={{0,1},{1,2},{2,3},{3,4},{4,5},{5,6},{6,7},{7,8},{8,9},{9,10},{10,1... | collective-permute-start | bytes 3145736 | tf_op jit(solution)/shard_map/ppermute | solution.py:15
  131.6 45.2 %collective-permute-start.12 = (f32[256,1024]{1,0:T(8,128)S(1)}, f32[256,1024]{1,0:T(8,128)S(1)}, u32[]{:S(2)}, u32[]{:S(2)}) collective-permute-start(f32[256,1024]{1,0:T(8,128)S(1)} %get-tuple-element.22), channel_id=1, source_target_pairs={{1,0},{2,1},{3,2},{4,3},{5,4},{6,5},{7,6},{8,7},{9,8},{10,9},{11,1... | collective-permute-start | bytes 3145736 | tf_op jit(solution)/shard_map/ppermute | solution.py:15
  134.1 42.7 %collective-permute-start.13 = (f32[256,1024]{1,0:T(8,128)S(1)}, f32[256,1024]{1,0:T(8,128)S(1)}, u32[]{:S(2)}, u32[]{:S(2)}) collective-permute-start(f32[256,1024]{1,0:T(8,128)S(1)} %get-tuple-element.23), channel_id=1, source_target_pairs={{1,0},{2,1},{3,2},{4,3},{5,4},{6,5},{7,6},{8,7},{9,8},{10,9},{11,1... | collective-permute-start | bytes 3145736 | tf_op jit(solution)/shard_map/ppermute | solution.py:15
  179.6 38.6 %collective-permute-start.6 = (f32[256,1024]{1,0:T(8,128)S(1)}, f32[256,1024]{1,0:T(8,128)S(1)}, u32[]{:S(2)}, u32[]{:S(2)}) collective-permute-start(f32[256,1024]{1,0:T(8,128)S(1)} %get-tuple-element.28), channel_id=1, source_target_pairs={{0,1},{1,2},{2,3},{3,4},{4,5},{5,6},{6,7},{7,8},{8,9},{9,10},{10,1... | collective-permute-start | bytes 3145736 | tf_op jit(solution)/shard_map/ppermute | solution.py:15
  184.0 45.4 %collective-permute-start.7 = (f32[256,1024]{1,0:T(8,128)S(1)}, f32[256,1024]{1,0:T(8,128)S(1)}, u32[]{:S(2)}, u32[]{:S(2)}) collective-permute-start(f32[256,1024]{1,0:T(8,128)S(1)} %get-tuple-element.29), channel_id=1, source_target_pairs={{0,1},{1,2},{2,3},{3,4},{4,5},{5,6},{6,7},{7,8},{8,9},{9,10},{10,1... | collective-permute-start | bytes 3145736 | tf_op jit(solution)/shard_map/ppermute | solution.py:15
  186.5 43.4 %collective-permute-start.14 = (f32[256,1024]{1,0:T(8,128)S(1)}, f32[256,1024]{1,0:T(8,128)S(1)}, u32[]{:S(2)}, u32[]{:S(2)}) collective-permute-start(f32[256,1024]{1,0:T(8,128)S(1)} %get-tuple-element.20), channel_id=1, source_target_pairs={{1,0},{2,1},{3,2},{4,3},{5,4},{6,5},{7,6},{8,7},{9,8},{10,9},{11,1... | collective-permute-start | bytes 3145736 | tf_op jit(solution)/shard_map/ppermute | solution.py:15
  188.9 40.9 %copy-start.2 = (f32[1,512,1024]{2,1,0:T(8,128)S(1)}, f32[1,512,1024]{2,1,0:T(8,128)}, u32[]{:S(2)}) copy-start(f32[1,512,1024]{2,1,0:T(8,128)} %param.6) | copy-start | bytes 6291460
  189.0 40.9 %collective-permute-start.15 = (f32[256,1024]{1,0:T(8,128)S(1)}, f32[256,1024]{1,0:T(8,128)S(1)}, u32[]{:S(2)}, u32[]{:S(2)}) collective-permute-start(f32[256,1024]{1,0:T(8,128)S(1)} %get-tuple-element.21), channel_id=1, source_target_pairs={{1,0},{2,1},{3,2},{4,3},{5,4},{6,5},{7,6},{8,7},{9,8},{10,9},{11,1... | collective-permute-start | bytes 3145736 | tf_op jit(solution)/shard_map/ppermute | solution.py:15
where the time goes:
time: 239 us; the launch traced here: 238 us
  waiting for transfers between devices  154 us (64%)
  starting transfers between devices  44.3 us (19%)
  matrix products  23.2 us (10%)
  other arithmetic  13 us (5%)
  local copies, waits for them, and re-layouts  2.54 us (1%)
    ppermute x16, waiting for transfers between devices, passed_along(): return lax.ppermute(block, axis, route)  154 us
    ppermute x16, starting transfers between devices, passed_along(): return lax.ppermute(block, axis, route)  44.3 us
    dot_general x9, matrix products, layer_terms(): lax.dot_general(pre_grad, weight, (((1,), (1,)), ((), ())), preferred_ele...  10.8 us
    dot_general x9, matrix products, layer_terms(): preact = jnp.dot(scaled, weight, preferred_element_type=jnp.float32)  9.66 us
  transfers between devices with their start and end apart: 16, of which 8 were waited for; matrix products, arithmetic and copies ran while one was open for 4% of the time, Pallas kernels for 0%

commit v1 on v0

v1 whole, which is shorter than its diff:
```python
import jax
import jax.numpy as jnp
from jax import lax
from jax.experimental import pallas as pl
from jax.experimental.pallas import tpu as pltpu
from jax.sharding import PartitionSpec as P


SWEEPS = 4
SHIFTS = (-16, 16)
CHUNKS = len(SHIFTS)

eps = 1e-06


def passed_along(block, axis, distance):
    devices = range(lax.axis_size(axis))
    route = [(i - distance, i) for i in devices if i - distance in devices]
    return lax.ppermute(block, axis, route)


def tick_kernel(x_ref, o_ref):
    o_ref[...] = x_ref[...]


def tick(x):
    return pl.pallas_call(
        tick_kernel,
        out_shape=jax.ShapeDtypeStruct(x.shape, x.dtype),
        in_specs=[pl.BlockSpec(memory_space=pltpu.VMEM)],
        out_specs=pl.BlockSpec(memory_space=pltpu.VMEM),
        name="tick",
    )(x)


def forward_terms(state, gain, weight):
    inverse = lax.rsqrt(jnp.mean(state * state, axis=-1, keepdims=True) + eps)
    normed = state * inverse
    scaled = (normed * gain).astype(jnp.bfloat16)
    preact = jnp.dot(scaled, weight, preferred_element_type=jnp.float32)
    return inverse, normed, scaled, preact, jax.nn.sigmoid(preact)


def backward_terms(adjoint, preact, squash, weight):
    pre_grad = (adjoint * squash * (1.0 + preact * (1.0 - squash))).astype(jnp.bfloat16)
    feat_grad = lax.dot_general(
        pre_grad, weight, (((1,), (1,)), ((), ())), preferred_element_type=jnp.float32
    )
    return pre_grad, feat_grad


def on_device(weights, gains, states, adjoints):
    weight = weights[0]
    turn = gains
    count = lax.axis_size("depth")
    index = lax.axis_index("depth")
    is_first = index == 0
    is_last = index == count - 1
    rows = [states.shape[1] // CHUNKS + shift for shift in SHIFTS]
    cuts = [sum(rows[:c]) for c in range(CHUNKS + 1)]
    start_states = [states[0, cuts[c] : cuts[c + 1]] for c in range(CHUNKS)]
    start_adjoints = [adjoints[0, cuts[c] : cuts[c + 1]] for c in range(CHUNKS)]
    state = list(start_states)
    adjoint = list(start_adjoints)
    for _ in range(SWEEPS):
        for c in range(CHUNKS):
            s, a, turn = lax.optimization_barrier((state[c], adjoint[c], turn))
            inverse, normed, scaled, preact, squash = forward_terms(s, turn, weight)
            output = s + preact * squash
            pre_grad, feat_grad = backward_terms(a, preact, squash, weight)
            gained = feat_grad * turn
            carried = a + inverse * (
                gained - normed * jnp.mean(gained * normed, axis=-1, keepdims=True)
            )
            output, carried, turn = lax.optimization_barrier((output, carried, turn))
            arrived = passed_along(output, "depth", 1)
            arrived_adjoint = passed_along(carried, "depth", -1)
            turn = tick(turn)
            state[c] = jnp.where(is_first, start_states[c], arrived)
            adjoint[c] = jnp.where(is_last, start_adjoints[c], arrived_adjoint)
    total = 0.0
    gain_total = 0.0
    for c in range(CHUNKS):
        s, a, turn = lax.optimization_barrier((state[c], adjoint[c], turn))
        inverse, normed, scaled, preact, squash = forward_terms(s, turn, weight)
        pre_grad, feat_grad = backward_terms(a, preact, squash, weight)
        total = total + lax.dot_general(
            scaled, pre_grad, (((0,), (0,)), ((), ())), preferred_element_type=jnp.float32
        )
        gain_total = gain_total + jnp.sum(normed * feat_grad, axis=0)
        total, turn, gain_total = lax.optimization_barrier((total, turn, gain_total))
        if c < CHUNKS - 1:
            turn = tick(turn)
    return (total.astype(jnp.bfloat16)[None], gain_total[None])


def solution(mesh):
    placed = (
        P("depth", None, None),
        P("depth", None),
        P("depth", None, None),
        P("depth", None, None),
    )
    return jax.shard_map(
        on_device,
        mesh=mesh,
        in_specs=placed,
        out_specs=(P("depth", None, None), P("depth", None)),
        check_vma=False,
    )
```

time: 239 us -> 218 us (0.912)
  the two profiles are of different devices: /device:TPU:1 before, /device:TPU:11 now
where the time goes in v1:
time: 218 us; the launch traced here: 217 us
  starting transfers between devices  67.3 us (31%)
  waiting for transfers between devices  66.5 us (31%)
  other arithmetic  39.5 us (18%)
  matrix products  24.4 us (11%)
  Pallas kernels  11.5 us (5%)
  local copies, waits for them, and re-layouts  6.41 us (3%)
    ppermute x16, starting transfers between devices, passed_along(): return lax.ppermute(block, axis, route)  67.3 us
    ppermute x16, waiting for transfers between devices, passed_along(): return lax.ppermute(block, axis, route)  66.5 us
    select_n x8, other arithmetic, on_device(): state[c] = jnp.where(is_first, start_states[c], arrived)  13.5 us
    add x8, other arithmetic, on_device(): a + inverse * (gained - normed * jnp.mean(gained * normed, axis=-1, keepd...  12.7 us
    pallas_call x9, Pallas kernels, tick(): pl.pallas_call(tick_kernel, out_shape=jax.ShapeDtypeStruct(x.shape, x.dty...  11.5 us
    select_n x8, other arithmetic, on_device(): adjoint[c] = jnp.where(is_last, start_adjoints[c], arrived_adjoint)  11 us
    dot_general x10, matrix products, backward_terms(): lax.dot_general(pre_grad, weight, (((1,), (1,)), ((), ())), preferred_ele...  10.7 us
    dot_general x10, matrix products, forward_terms(): preact = jnp.dot(scaled, weight, preferred_element_type=jnp.float32)  8.17 us
  transfers between devices with their start and end apart: 16, of which 9 were waited for; matrix products, arithmetic and copies ran while one was open for 25% of the time, Pallas kernels for 5%

profile of v1, /device:TPU:11, one launch (start us, length us, event | category | flops | bytes accessed | tf_op | source)
XLA Modules:
  0.0 216.7 jit_solution(10439826035608434158)
XLA Ops:
  0.7 1.8 slice_bitcast_fusion.2
  6.3 3.8 %collective-permute-start = (f32[240,1024]{1,0:T(8,128)}, f32[240,1024]{1,0:T(8,128)}, u32[]{:S(2)}, u32[]{:S(2)}) collective-permute-start(f32[240,1024]{1,0:T(8,128)} %get-tuple-element.64), channel_id=1, source_target_pairs={{0,1},{1,2},{2,3},{3,4},{4,5},{5,6},{6,7},{7,8},{8,9},{9,10},{10,1... | collective-permute-start | bytes 2949128 | tf_op jit(solution)/shard_map/ppermute | solution.py:19
  10.1 1.9 collective-permute-start.1
  17.6 1.8 multiply_add_fusion.6
  19.4 4.5 %collective-permute-start.4 = (f32[272,1024]{1,0:T(8,128)}, f32[272,1024]{1,0:T(8,128)}, u32[]{:S(2)}, u32[]{:S(2)}) collective-permute-start(f32[272,1024]{1,0:T(8,128)} %get-tuple-element.76), channel_id=1, source_target_pairs={{0,1},{1,2},{2,3},{3,4},{4,5},{5,6},{6,7},{7,8},{8,9},{9,10},{10,1... | collective-permute-start | bytes 3342344 | tf_op jit(solution)/shard_map/ppermute | solution.py:19
  24.0 1.9 collective-permute-start.5
  27.2 2.0 collective-permute-done
  30.9 6.4 %collective-permute-done.1 = f32[240,1024]{1,0:T(8,128)} collective-permute-done((f32[240,1024]{1,0:T(8,128)}, f32[240,1024]{1,0:T(8,128)}, u32[]{:S(2)}, u32[]{:S(2)}) %collective-permute-start.1) | collective-permute-done | bytes 983072 | tf_op jit(solution)/shard_map/ppermute | solution.py:19
  43.8 2.0 collective-permute-start.2
  45.9 11.6 %collective-permute-start.3 = (f32[240,1024]{1,0:T(8,128)}, f32[240,1024]{1,0:T(8,128)}, u32[]{:S(2)}, u32[]{:S(2)}) collective-permute-start(f32[240,1024]{1,0:T(8,128)} %get-tuple-element.75), channel_id=1, source_target_pairs={{1,0},{2,1},{3,2},{4,3},{5,4},{6,5},{7,6},{8,7},{9,8},{10,9},{11,1... | collective-permute-start | bytes 2949128 | tf_op jit(solution)/shard_map/ppermute | solution.py:19
  57.5 1.7 broadcast_select_fusion.7
  64.8 12.8 %collective-permute-start.8 = (f32[272,1024]{1,0:T(8,128)}, f32[272,1024]{1,0:T(8,128)}, u32[]{:S(2)}, u32[]{:S(2)}) collective-permute-start(f32[272,1024]{1,0:T(8,128)} %get-tuple-element.88), channel_id=1, source_target_pairs={{0,1},{1,2},{2,3},{3,4},{4,5},{5,6},{6,7},{7,8},{8,9},{9,10},{10,1... | collective-permute-start | bytes 3342344 | tf_op jit(solution)/shard_map/ppermute | solution.py:19
  77.7 1.9 collective-permute-start.9
  81.3 9.7 %collective-permute-done.3 = f32[240,1024]{1,0:T(8,128)} collective-permute-done((f32[240,1024]{1,0:T(8,128)}, f32[240,1024]{1,0:T(8,128)}, u32[]{:S(2)}, u32[]{:S(2)}) %collective-permute-start.3) | collective-permute-done | bytes 983072 | tf_op jit(solution)/shard_map/ppermute | solution.py:19
  97.5 2.0 collective-permute-start.6
  99.6 2.6 %collective-permute-start.7 = (f32[240,1024]{1,0:T(8,128)}, f32[240,1024]{1,0:T(8,128)}, u32[]{:S(2)}, u32[]{:S(2)}) collective-permute-start(f32[240,1024]{1,0:T(8,128)} %get-tuple-element.87), channel_id=1, source_target_pairs={{1,0},{2,1},{3,2},{4,3},{5,4},{6,5},{7,6},{8,7},{9,8},{10,9},{11,1... | collective-permute-start | bytes 2949128 | tf_op jit(solution)/shard_map/ppermute | solution.py:19
  102.2 1.7 broadcast_select_fusion.6
  103.9 8.3 %collective-permute-done.9 = f32[272,1024]{1,0:T(8,128)} collective-permute-done((f32[272,1024]{1,0:T(8,128)S(1)}, f32[272,1024]{1,0:T(8,128)}, u32[]{:S(2)}, u32[]{:S(2)}) %collective-permute-start.9) | collective-permute-done | bytes 1114144 | tf_op jit(solution)/shard_map/ppermute | solution.py:19
  119.1 6.3 %collective-permute-start.12 = (f32[272,1024]{1,0:T(8,128)}, f32[272,1024]{1,0:T(8,128)}, u32[]{:S(2)}, u32[]{:S(2)}) collective-permute-start(f32[272,1024]{1,0:T(8,128)} %get-tuple-element.100), channel_id=1, source_target_pairs={{0,1},{1,2},{2,3},{3,4},{4,5},{5,6},{6,7},{7,8},{8,9},{9,10},{10,1... | collective-permute-start | bytes 3342344 | tf_op jit(solution)/shard_map/ppermute | solution.py:19
  125.4 1.9 collective-permute-start.13
  129.0 5.7 %collective-permute-done.7 = f32[240,1024]{1,0:T(8,128)} collective-permute-done((f32[240,1024]{1,0:T(8,128)}, f32[240,1024]{1,0:T(8,128)}, u32[]{:S(2)}, u32[]{:S(2)}) %collective-permute-start.7) | collective-permute-done | bytes 983072 | tf_op jit(solution)/shard_map/ppermute | solution.py:19
  141.2 7.5 %collective-permute-start.10 = (f32[240,1024]{1,0:T(8,128)}, f32[240,1024]{1,0:T(8,128)}, u32[]{:S(2)}, u32[]{:S(2)}) collective-permute-start(f32[240,1024]{1,0:T(8,128)} %get-tuple-element.98), channel_id=1, source_target_pairs={{0,1},{1,2},{2,3},{3,4},{4,5},{5,6},{6,7},{7,8},{8,9},{9,10},{10,1... | collective-permute-start | bytes 2949128 | tf_op jit(solution)/shard_map/ppermute | solution.py:19
  148.7 1.9 collective-permute-start.11
  150.7 1.7 broadcast_select_fusion.5
  152.4 11.2 %collective-permute-done.13 = f32[272,1024]{1,0:T(8,128)} collective-permute-done((f32[272,1024]{1,0:T(8,128)S(1)}, f32[272,1024]{1,0:T(8,128)}, u32[]{:S(2)}, u32[]{:S(2)}) %collective-permute-start.13) | collective-permute-done | bytes 1114144 | tf_op jit(solution)/shard_map/ppermute | solution.py:19
  170.5 1.9 collective-permute-start.14
  172.4 2.6 %collective-permute-start.15 = (f32[272,1024]{1,0:T(8,128)S(1)}, f32[272,1024]{1,0:T(8,128)}, u32[]{:S(2)}, u32[]{:S(2)}) collective-permute-start(f32[272,1024]{1,0:T(8,128)S(1)} %get-tuple-element.112), channel_id=1, source_target_pairs={{1,0},{2,1},{3,2},{4,3},{5,4},{6,5},{7,6},{8,7},{9,8},{10,9},{11,1... | collective-permute-start | bytes 3342344 | tf_op jit(solution)/shard_map/ppermute | solution.py:19
  176.7 5.6 %collective-permute-done.11 = f32[240,1024]{1,0:T(8,128)} collective-permute-done((f32[240,1024]{1,0:T(8,128)}, f32[240,1024]{1,0:T(8,128)}, u32[]{:S(2)}, u32[]{:S(2)}) %collective-permute-start.11) | collective-permute-done | bytes 983072 | tf_op jit(solution)/shard_map/ppermute | solution.py:19
  185.9 2.8 %fusion.108 = f32[1024,1024]{1,0:T(8,128)} fusion(bf16[240,1024]{1,0:T(8,128)(2,1)S(1)} %multiply_convert_fusion.10, f32[240,1024]{1,0:T(8,128)S(1)} %broadcast_select_fusion.12, f32[1024]{0:T(1024)S(1)} %bitcast.159, f32[240]{0:T(256)S(1)} %add_rsqrt_fusion.5), kind=kOutput, calls=%fused_computation.186 | convolution fusion | flops 504053760 | bytes 5673920 | tf_op jit(solution)/shard_map/dot_general | solution.py:87
  189.9 4.8 %collective-permute-done.14 = f32[272,1024]{1,0:T(8,128)} collective-permute-done((f32[272,1024]{1,0:T(8,128)}, f32[272,1024]{1,0:T(8,128)}, u32[]{:S(2)}, u32[]{:S(2)}) %collective-permute-start.14) | collective-permute-done | bytes 1114144 | tf_op jit(solution)/shard_map/ppermute | solution.py:19
  196.4 12.6 %collective-permute-done.15 = f32[272,1024]{1,0:T(8,128)} collective-permute-done((f32[272,1024]{1,0:T(8,128)S(1)}, f32[272,1024]{1,0:T(8,128)}, u32[]{:S(2)}, u32[]{:S(2)}) %collective-permute-start.15) | collective-permute-done | bytes 1114144 | tf_op jit(solution)/shard_map/ppermute | solution.py:19
  213.4 2.8 %convolution_add_fusion = bf16[1024,1024]{1,0:T(8,128)(2,1)} fusion(f32[1024,1024]{1,0:T(8,128)S(1)} %copy-done.7, bf16[272,1024]{1,0:T(8,128)(2,1)S(1)} %multiply_convert_fusion, f32[272,1024]{1,0:T(8,128)S(1)} %broadcast_select_fusion.4, f32[1024]{0:T(1024)S(1)} %bitcast.161, f32[272]{0:T(512)S(1)} %add_rsqrt_fusion), kind=kOutput, calls=%fused_computation | convolution fusion | flops 573358080 | bytes 7967808 | tf_op jit(solution)/shard_map/dot_general | solution.py:87
  (124 shorter events, 67.4 us)
Async XLA Ops:
  0.6 2.2 %copy-start = (bf16[1,1024,1024]{2,1,0:T(8,128)(2,1)S(1)}, bf16[1,1024,1024]{2,1,0:T(8,128)(2,1)}, u32[]{:S(2)}) copy-start(bf16[1,1024,1024]{2,1,0:T(8,128)(2,1)} %param.4) | copy-start | bytes 6291460
  0.6 2.2 %copy-start.18 = (f32[1,1024]{1,0:T(1,128)S(1)}, f32[1,1024]{1,0:T(1,128)}, u32[]{:S(2)}) copy-start(f32[1,1024]{1,0:T(1,128)} %x_ref) | copy-start | bytes 12292
  4.6 7.4 %copy-start.1 = (f32[1,512,1024]{2,1,0:T(8,128)S(1)}, f32[1,512,1024]{2,1,0:T(8,128)}, u32[]{:S(2)}) copy-start(f32[1,512,1024]{2,1,0:T(8,128)} %param.6) | copy-start | bytes 6291460
  4.7 7.4 %copy-start.2 = (f32[1,512,1024]{2,1,0:T(8,128)S(1)}, f32[1,512,1024]{2,1,0:T(8,128)}, u32[]{:S(2)}) copy-start(f32[1,512,1024]{2,1,0:T(8,128)} %param.7) | copy-start | bytes 6291460
  6.3 22.9 %collective-permute-start = (f32[240,1024]{1,0:T(8,128)}, f32[240,1024]{1,0:T(8,128)}, u32[]{:S(2)}, u32[]{:S(2)}) collective-permute-start(f32[240,1024]{1,0:T(8,128)} %get-tuple-element.64), channel_id=1, source_target_pairs={{0,1},{1,2},{2,3},{3,4},{4,5},{5,6},{6,7},{7,8},{8,9},{9,10},{10,1... | collective-permute-start | bytes 2949128 | tf_op jit(solution)/shard_map/ppermute | solution.py:19
  10.1 27.2 %collective-permute-start.1 = (f32[240,1024]{1,0:T(8,128)}, f32[240,1024]{1,0:T(8,128)}, u32[]{:S(2)}, u32[]{:S(2)}) collective-permute-start(f32[240,1024]{1,0:T(8,128)} %get-tuple-element.65), channel_id=1, source_target_pairs={{1,0},{2,1},{3,2},{4,3},{5,4},{6,5},{7,6},{8,7},{9,8},{10,9},{11,1... | collective-permute-start | bytes 2949128 | tf_op jit(solution)/shard_map/ppermute | solution.py:19
  15.2 1.2 copy-start.8
  19.4 38.0 %collective-permute-start.4 = (f32[272,1024]{1,0:T(8,128)}, f32[272,1024]{1,0:T(8,128)}, u32[]{:S(2)}, u32[]{:S(2)}) collective-permute-start(f32[272,1024]{1,0:T(8,128)} %get-tuple-element.76), channel_id=1, source_target_pairs={{0,1},{1,2},{2,3},{3,4},{4,5},{5,6},{6,7},{7,8},{8,9},{9,10},{10,1... | collective-permute-start | bytes 3342344 | tf_op jit(solution)/shard_map/ppermute | solution.py:19
  24.0 35.3 %collective-permute-start.5 = (f32[272,1024]{1,0:T(8,128)}, f32[272,1024]{1,0:T(8,128)S(1)}, u32[]{:S(2)}, u32[]{:S(2)}) collective-permute-start(f32[272,1024]{1,0:T(8,128)} %get-tuple-element.77), channel_id=1, source_target_pairs={{1,0},{2,1},{3,2},{4,3},{5,4},{6,5},{7,6},{8,7},{9,8},{10,9},{11,1... | collective-permute-start | bytes 3342344 | tf_op jit(solution)/shard_map/ppermute | solution.py:19
  30.9 8.2 %copy-start.15 = (f32[1,1024]{1,0:T(1,128)S(1)}, f32[1,1024]{1,0:T(1,128)}, u32[]{:S(2)}) copy-start(f32[1,1024]{1,0:T(1,128)} %tick.10.x_ref) | copy-start | bytes 12292
  43.8 15.4 %copy-start.3 = (f32[1,512,1024]{2,1,0:T(8,128)S(1)}, f32[1,512,1024]{2,1,0:T(8,128)}, u32[]{:S(2)}) copy-start(f32[1,512,1024]{2,1,0:T(8,128)} %param.7) | copy-start | bytes 6291460
  43.8 35.8 %collective-permute-start.2 = (f32[240,1024]{1,0:T(8,128)}, f32[240,1024]{1,0:T(8,128)}, u32[]{:S(2)}, u32[]{:S(2)}) collective-permute-start(f32[240,1024]{1,0:T(8,128)} %get-tuple-element.74), channel_id=1, source_target_pairs={{0,1},{1,2},{2,3},{3,4},{4,5},{5,6},{6,7},{7,8},{8,9},{9,10},{10,1... | collective-permute-start | bytes 2949128 | tf_op jit(solution)/shard_map/ppermute | solution.py:19
  45.9 45.1 %collective-permute-start.3 = (f32[240,1024]{1,0:T(8,128)}, f32[240,1024]{1,0:T(8,128)}, u32[]{:S(2)}, u32[]{:S(2)}) collective-permute-start(f32[240,1024]{1,0:T(8,128)} %get-tuple-element.75), channel_id=1, source_target_pairs={{1,0},{2,1},{3,2},{4,3},{5,4},{6,5},{7,6},{8,7},{9,8},{10,9},{11,1... | collective-permute-start | bytes 2949128 | tf_op jit(solution)/shard_map/ppermute | solution.py:19
  59.4 0.7 copy-start.9
  64.8 37.3 %collective-permute-start.8 = (f32[272,1024]{1,0:T(8,128)}, f32[272,1024]{1,0:T(8,128)}, u32[]{:S(2)}, u32[]{:S(2)}) collective-permute-start(f32[272,1024]{1,0:T(8,128)} %get-tuple-element.88), channel_id=1, source_target_pairs={{0,1},{1,2},{2,3},{3,4},{4,5},{5,6},{6,7},{7,8},{8,9},{9,10},{10,1... | collective-permute-start | bytes 3342344 | tf_op jit(solution)/shard_map/ppermute | solution.py:19
  77.7 34.6 %collective-permute-start.9 = (f32[272,1024]{1,0:T(8,128)S(1)}, f32[272,1024]{1,0:T(8,128)}, u32[]{:S(2)}, u32[]{:S(2)}) collective-permute-start(f32[272,1024]{1,0:T(8,128)S(1)} %get-tuple-element.89), channel_id=1, source_target_pairs={{1,0},{2,1},{3,2},{4,3},{5,4},{6,5},{7,6},{8,7},{9,8},{10,9},{11,1... | collective-permute-start | bytes 3342344 | tf_op jit(solution)/shard_map/ppermute | solution.py:19
  81.3 11.5 %copy-start.13 = (f32[1,1024]{1,0:T(1,128)S(1)}, f32[1,1024]{1,0:T(1,128)}, u32[]{:S(2)}) copy-start(f32[1,1024]{1,0:T(1,128)} %tick.12.x_ref) | copy-start | bytes 12292
  97.5 14.7 %copy-start.4 = (f32[1,512,1024]{2,1,0:T(8,128)S(1)}, f32[1,512,1024]{2,1,0:T(8,128)}, u32[]{:S(2)}) copy-start(f32[1,512,1024]{2,1,0:T(8,128)} %param.7) | copy-start | bytes 6291460
  97.5 29.8 %collective-permute-start.6 = (f32[240,1024]{1,0:T(8,128)}, f32[240,1024]{1,0:T(8,128)}, u32[]{:S(2)}, u32[]{:S(2)}) collective-permute-start(f32[240,1024]{1,0:T(8,128)} %get-tuple-element.86), channel_id=1, source_target_pairs={{0,1},{1,2},{2,3},{3,4},{4,5},{5,6},{6,7},{7,8},{8,9},{9,10},{10,1... | collective-permute-start | bytes 2949128 | tf_op jit(solution)/shard_map/ppermute | solution.py:19
  99.6 35.1 %collective-permute-start.7 = (f32[240,1024]{1,0:T(8,128)}, f32[240,1024]{1,0:T(8,128)}, u32[]{:S(2)}, u32[]{:S(2)}) collective-permute-start(f32[240,1024]{1,0:T(8,128)} %get-tuple-element.87), channel_id=1, source_target_pairs={{1,0},{2,1},{3,2},{4,3},{5,4},{6,5},{7,6},{8,7},{9,8},{10,9},{11,1... | collective-permute-start | bytes 2949128 | tf_op jit(solution)/shard_map/ppermute | solution.py:19
  113.7 0.7 copy-start.10
  119.1 31.5 %collective-permute-start.12 = (f32[272,1024]{1,0:T(8,128)}, f32[272,1024]{1,0:T(8,128)}, u32[]{:S(2)}, u32[]{:S(2)}) collective-permute-start(f32[272,1024]{1,0:T(8,128)} %get-tuple-element.100), channel_id=1, source_target_pairs={{0,1},{1,2},{2,3},{3,4},{4,5},{5,6},{6,7},{7,8},{8,9},{9,10},{10,1... | collective-permute-start | bytes 3342344 | tf_op jit(solution)/shard_map/ppermute | solution.py:19
  125.4 38.2 %collective-permute-start.13 = (f32[272,1024]{1,0:T(8,128)S(1)}, f32[272,1024]{1,0:T(8,128)}, u32[]{:S(2)}, u32[]{:S(2)}) collective-permute-start(f32[272,1024]{1,0:T(8,128)S(1)} %get-tuple-element.101), channel_id=1, source_target_pairs={{1,0},{2,1},{3,2},{4,3},{5,4},{6,5},{7,6},{8,7},{9,8},{10,9},{11,1... | collective-permute-start | bytes 3342344 | tf_op jit(solution)/shard_map/ppermute | solution.py:19
  129.0 7.5 %copy-start.14 = (f32[1,1024]{1,0:T(1,128)S(1)}, f32[1,1024]{1,0:T(1,128)}, u32[]{:S(2)}) copy-start(f32[1,1024]{1,0:T(1,128)} %tick.14.x_ref) | copy-start | bytes 12292
  141.2 22.4 %copy-start.5 = (f32[1,512,1024]{2,1,0:T(8,128)S(1)}, f32[1,512,1024]{2,1,0:T(8,128)}, u32[]{:S(2)}) copy-start(f32[1,512,1024]{2,1,0:T(8,128)} %param.7) | copy-start | bytes 6291460
  141.2 33.8 %collective-permute-start.10 = (f32[240,1024]{1,0:T(8,128)}, f32[240,1024]{1,0:T(8,128)}, u32[]{:S(2)}, u32[]{:S(2)}) collective-permute-start(f32[240,1024]{1,0:T(8,128)} %get-tuple-element.98), channel_id=1, source_target_pairs={{0,1},{1,2},{2,3},{3,4},{4,5},{5,6},{6,7},{7,8},{8,9},{9,10},{10,1... | collective-permute-start | bytes 2949128 | tf_op jit(solution)/shard_map/ppermute | solution.py:19
  148.7 33.6 %collective-permute-start.11 = (f32[240,1024]{1,0:T(8,128)}, f32[240,1024]{1,0:T(8,128)}, u32[]{:S(2)}, u32[]{:S(2)}) collective-permute-start(f32[240,1024]{1,0:T(8,128)} %get-tuple-element.99), channel_id=1, source_target_pairs={{1,0},{2,1},{3,2},{4,3},{5,4},{6,5},{7,6},{8,7},{9,8},{10,9},{11,1... | collective-permute-start | bytes 2949128 | tf_op jit(solution)/shard_map/ppermute | solution.py:19
  170.5 24.2 %collective-permute-start.14 = (f32[272,1024]{1,0:T(8,128)}, f32[272,1024]{1,0:T(8,128)}, u32[]{:S(2)}, u32[]{:S(2)}) collective-permute-start(f32[272,1024]{1,0:T(8,128)} %get-tuple-element.111), channel_id=1, source_target_pairs={{0,1},{1,2},{2,3},{3,4},{4,5},{5,6},{6,7},{7,8},{8,9},{9,10},{10,1... | collective-permute-start | bytes 3342344 | tf_op jit(solution)/shard_map/ppermute | solution.py:19
  172.4 36.6 %collective-permute-start.15 = (f32[272,1024]{1,0:T(8,128)S(1)}, f32[272,1024]{1,0:T(8,128)}, u32[]{:S(2)}, u32[]{:S(2)}) collective-permute-start(f32[272,1024]{1,0:T(8,128)S(1)} %get-tuple-element.112), channel_id=1, source_target_pairs={{1,0},{2,1},{3,2},{4,3},{5,4},{6,5},{7,6},{8,7},{9,8},{10,9},{11,1... | collective-permute-start | bytes 3342344 | tf_op jit(solution)/shard_map/ppermute | solution.py:19
  176.7 7.4 %copy-start.16 = (f32[1,1024]{1,0:T(1,128)S(1)}, f32[1,1024]{1,0:T(1,128)}, u32[]{:S(2)}) copy-start(f32[1,1024]{1,0:T(1,128)} %tick.16.x_ref) | copy-start | bytes 12292
  189.9 19.1 %copy-start.6 = (f32[1,512,1024]{2,1,0:T(8,128)S(1)}, f32[1,512,1024]{2,1,0:T(8,128)}, u32[]{:S(2)}) copy-start(f32[1,512,1024]{2,1,0:T(8,128)} %param.7) | copy-start | bytes 6291460
  211.2 2.2 %copy-start.7 = (f32[1024,1024]{1,0:T(8,128)S(1)}, f32[1024,1024]{1,0:T(8,128)}, u32[]{:S(2)}) copy-start(f32[1024,1024]{1,0:T(8,128)} %fusion.108) | copy-start | bytes 12582916
  (3 other events, 2.1 us)

commit v2 on v1

--- a/solution.py
+++ b/solution.py
@@ -7,15 +7,17 @@
 
 
 SWEEPS = 4
-SHIFTS = (-16, 16)
-CHUNKS = len(SHIFTS)
+SHARES = (8, 14, 10)
+CHUNKS = len(SHARES)
 
 eps = 1e-06
 
 
-def passed_along(block, axis, distance):
-    devices = range(lax.axis_size(axis))
-    route = [(i - distance, i) for i in devices if i - distance in devices]
+def swapped(block, axis, first):
+    count = lax.axis_size(axis)
+    route = []
+    for i in range(first, count - 1, 2):
+        route += [(i, i + 1), (i + 1, i)]
     return lax.ppermute(block, axis, route)
 
 
@@ -30,6 +32,7 @@
         in_specs=[pl.BlockSpec(memory_space=pltpu.VMEM)],
         out_specs=pl.BlockSpec(memory_space=pltpu.VMEM),
         name="tick",
+        compiler_params=pltpu.CompilerParams(vmem_limit_bytes=256 * 1024),
     )(x)
 
 
@@ -56,7 +59,9 @@
     index = lax.axis_index("depth")
     is_first = index == 0
     is_last = index == count - 1
-    rows = [states.shape[1] // CHUNKS + shift for shift in SHIFTS]
+    is_even = index % 2 == 0
+    unit = states.shape[1] // sum(SHARES)
+    rows = [share * unit for share in SHARES]
     cuts = [sum(rows[:c]) for c in range(CHUNKS + 1)]
     start_states = [states[0, cuts[c] : cuts[c + 1]] for c in range(CHUNKS)]
     start_adjoints = [adjoints[0, cuts[c] : cuts[c + 1]] for c in range(CHUNKS)]
@@ -72,12 +77,18 @@
             carried = a + inverse * (
                 gained - normed * jnp.mean(gained * normed, axis=-1, keepdims=True)
             )
-            output, carried, turn = lax.optimization_barrier((output, carried, turn))
-            arrived = passed_along(output, "depth", 1)
-            arrived_adjoint = passed_along(carried, "depth", -1)
+            near = jnp.where(is_even, output, carried)
+            far = jnp.where(is_even, carried, output)
+            near, far, turn = lax.optimization_barrier((near, far, turn))
+            near = swapped(near, "depth", 0)
+            far = swapped(far, "depth", 1)
             turn = tick(turn)
-            state[c] = jnp.where(is_first, start_states[c], arrived)
-            adjoint[c] = jnp.where(is_last, start_adjoints[c], arrived_adjoint)
+            state[c] = jnp.where(
+                is_first, start_states[c], jnp.where(is_even, far, near)
+            )
+            adjoint[c] = jnp.where(
+                is_last, start_adjoints[c], jnp.where(is_even, near, far)
+            )
     total = 0.0
     gain_total = 0.0
     for c in range(CHUNKS):
@@ -88,8 +99,8 @@
             scaled, pre_grad, (((0,), (0,)), ((), ())), preferred_element_type=jnp.float32
         )
         gain_total = gain_total + jnp.sum(normed * feat_grad, axis=0)
-        total, turn, gain_total = lax.optimization_barrier((total, turn, gain_total))
         if c < CHUNKS - 1:
+            total, turn, gain_total = lax.optimization_barrier((total, turn, gain_total))
             turn = tick(turn)
     return (total.astype(jnp.bfloat16)[None], gain_total[None])
 

time: 218 us -> 230 us (1.055)
  the two profiles are of different devices: /device:TPU:11 before, /device:TPU:1 now
where the time goes in v2:
time: 230 us
  waiting for transfers between devices  136 us (59%)
  starting transfers between devices  42.9 us (19%)
  matrix products  27.8 us (12%)
  other arithmetic  20 us (9%)
    ppermute x24, waiting for transfers between devices, swapped(): return lax.ppermute(block, axis, route)  136 us
    ppermute x24, starting transfers between devices, swapped(): return lax.ppermute(block, axis, route)  42.9 us
    dot_general x15, matrix products, backward_terms(): lax.dot_general(pre_grad, weight, (((1,), (1,)), ((), ())), preferred_ele...  14.6 us
    dot_general x15, matrix products, forward_terms(): preact = jnp.dot(scaled, weight, preferred_element_type=jnp.float32)  9.43 us
    select_n x12, other arithmetic, on_device(): far = jnp.where(is_even, carried, output)  6.68 us
    select_n x12, other arithmetic, on_device(): jnp.where(is_last, start_adjoints[c], jnp.where(is_even, near, far))  6.46 us
  transfers between devices with their start and end apart: 24, of which 11 were waited for; matrix products, arithmetic and copies ran while one was open for 10% of the time, Pallas kernels for 0%

profile of v2, /device:TPU:1, one launch (start us, length us, event | category | flops | bytes accessed | tf_op | source)
XLA Modules:
  0.0 229.7 jit_solution(1341009020671203024)
XLA Ops:
  0.7 1.4 slice_bitcast_fusion.4
  5.2 4.6 %collective-permute-start = (f32[128,1024]{1,0:T(8,128)}, f32[128,1024]{1,0:T(8,128)}, u32[]{:S(2)}, u32[]{:S(2)}) collective-permute-start(f32[128,1024]{1,0:T(8,128)} %get-tuple-element.92), channel_id=1, source_target_pairs={{1,2},{2,1},{3,4},{4,3},{5,6},{6,5},{7,8},{8,7},{9,10},{10,9},{11,... | collective-permute-start | bytes 1572872 | tf_op jit(solution)/shard_map/ppermute | solution.py:21
  12.1 1.3 broadcast_select_fusion.6
  13.5 1.2 broadcast_select_fusion.7
  16.4 1.2 broadcast_select_fusion.14
  18.7 3.5 %collective-permute-start.4 = (f32[160,1024]{1,0:T(8,128)}, f32[160,1024]{1,0:T(8,128)}, u32[]{:S(2)}, u32[]{:S(2)}) collective-permute-start(f32[160,1024]{1,0:T(8,128)} %get-tuple-element.108), channel_id=1, source_target_pairs={{1,2},{2,1},{3,4},{4,3},{5,6},{6,5},{7,8},{8,7},{9,10},{10,9},{11,... | collective-permute-start | bytes 1966088 | tf_op jit(solution)/shard_map/ppermute | solution.py:21
  22.2 3.5 %collective-permute-start.6 = (f32[224,1024]{1,0:T(8,128)}, f32[224,1024]{1,0:T(8,128)S(1)}, u32[]{:S(2)}, u32[]{:S(2)}) collective-permute-start(f32[224,1024]{1,0:T(8,128)} %get-tuple-element.110), channel_id=1, source_target_pairs={{1,2},{2,1},{3,4},{4,3},{5,6},{6,5},{7,8},{8,7},{9,10},{10,9},{11,... | collective-permute-start | bytes 2752520 | tf_op jit(solution)/shard_map/ppermute | solution.py:21
  25.8 1.7 select_select_fusion.22
  29.5 3.9 %collective-permute-start.2 = (f32[128,1024]{1,0:T(8,128)S(1)}, f32[128,1024]{1,0:T(8,128)S(1)}, u32[]{:S(2)}, u32[]{:S(2)}) collective-permute-start(f32[128,1024]{1,0:T(8,128)S(1)} %get-tuple-element.106), channel_id=1, source_target_pairs={{1,2},{2,1},{3,4},{4,3},{5,6},{6,5},{7,8},{8,7},{9,10},{10,9},{11,... | collective-permute-start | bytes 1572872 | tf_op jit(solution)/shard_map/ppermute | solution.py:21
  33.5 18.9 %collective-permute-done.4 = f32[160,1024]{1,0:T(8,128)} collective-permute-done((f32[160,1024]{1,0:T(8,128)}, f32[160,1024]{1,0:T(8,128)}, u32[]{:S(2)}, u32[]{:S(2)}) %collective-permute-start.4) | collective-permute-done | bytes 655392 | tf_op jit(solution)/shard_map/ppermute | solution.py:21
  52.4 1.5 select_select_fusion.14
  54.0 8.3 %collective-permute-done.6 = f32[224,1024]{1,0:T(8,128)S(1)} collective-permute-done((f32[224,1024]{1,0:T(8,128)}, f32[224,1024]{1,0:T(8,128)S(1)}, u32[]{:S(2)}, u32[]{:S(2)}) %collective-permute-start.6) | collective-permute-done | bytes 917536 | tf_op jit(solution)/shard_map/ppermute | solution.py:21
  63.6 1.1 multiply_reduce_fusion.5
  67.7 5.7 %collective-permute-done.2 = f32[128,1024]{1,0:T(8,128)S(1)} collective-permute-done((f32[128,1024]{1,0:T(8,128)S(1)}, f32[128,1024]{1,0:T(8,128)S(1)}, u32[]{:S(2)}, u32[]{:S(2)}) %collective-permute-start.2) | collective-permute-done | bytes 524320 | tf_op jit(solution)/shard_map/ppermute | solution.py:21
  75.6 4.4 %collective-permute-start.8 = (f32[128,1024]{1,0:T(8,128)S(1)}, f32[128,1024]{1,0:T(8,128)S(1)}, u32[]{:S(2)}, u32[]{:S(2)}) collective-permute-start(f32[128,1024]{1,0:T(8,128)S(1)} %get-tuple-element.124), channel_id=1, source_target_pairs={{1,2},{2,1},{3,4},{4,3},{5,6},{6,5},{7,8},{8,7},{9,10},{10,9},{11,... | collective-permute-start | bytes 1572872 | tf_op jit(solution)/shard_map/ppermute | solution.py:21
  80.1 1.9 collective-permute-start.10
  82.1 3.9 %collective-permute-start.12 = (f32[224,1024]{1,0:T(8,128)S(1)}, f32[224,1024]{1,0:T(8,128)S(1)}, u32[]{:S(2)}, u32[]{:S(2)}) collective-permute-start(f32[224,1024]{1,0:T(8,128)S(1)} %get-tuple-element.128), channel_id=1, source_target_pairs={{1,2},{2,1},{3,4},{4,3},{5,6},{6,5},{7,8},{8,7},{9,10},{10,9},{11,... | collective-permute-start | bytes 2752520 | tf_op jit(solution)/shard_map/ppermute | solution.py:21
  85.9 17.0 %collective-permute-done.8 = f32[128,1024]{1,0:T(8,128)S(1)} collective-permute-done((f32[128,1024]{1,0:T(8,128)S(1)}, f32[128,1024]{1,0:T(8,128)S(1)}, u32[]{:S(2)}, u32[]{:S(2)}) %collective-permute-start.8) | collective-permute-done | bytes 524320 | tf_op jit(solution)/shard_map/ppermute | solution.py:21
  103.2 6.8 %collective-permute-done.10 = f32[160,1024]{1,0:T(8,128)S(1)} collective-permute-done((f32[160,1024]{1,0:T(8,128)S(1)}, f32[160,1024]{1,0:T(8,128)S(1)}, u32[]{:S(2)}, u32[]{:S(2)}) %collective-permute-start.10) | collective-permute-done | bytes 655392 | tf_op jit(solution)/shard_map/ppermute | solution.py:21
  110.3 15.2 %collective-permute-done.12 = f32[224,1024]{1,0:T(8,128)S(1)} collective-permute-done((f32[224,1024]{1,0:T(8,128)S(1)}, f32[224,1024]{1,0:T(8,128)S(1)}, u32[]{:S(2)}, u32[]{:S(2)}) %collective-permute-start.12) | collective-permute-done | bytes 917536 | tf_op jit(solution)/shard_map/ppermute | solution.py:21
  132.9 4.4 %collective-permute-start.14 = (f32[128,1024]{1,0:T(8,128)S(1)}, f32[128,1024]{1,0:T(8,128)S(1)}, u32[]{:S(2)}, u32[]{:S(2)}) collective-permute-start(f32[128,1024]{1,0:T(8,128)S(1)} %get-tuple-element.142), channel_id=1, source_target_pairs={{1,2},{2,1},{3,4},{4,3},{5,6},{6,5},{7,8},{8,7},{9,10},{10,9},{11,... | collective-permute-start | bytes 1572872 | tf_op jit(solution)/shard_map/ppermute | solution.py:21
  137.4 1.9 collective-permute-start.16
  139.4 3.6 %collective-permute-start.18 = (f32[224,1024]{1,0:T(8,128)S(1)}, f32[224,1024]{1,0:T(8,128)S(1)}, u32[]{:S(2)}, u32[]{:S(2)}) collective-permute-start(f32[224,1024]{1,0:T(8,128)S(1)} %get-tuple-element.146), channel_id=1, source_target_pairs={{1,2},{2,1},{3,4},{4,3},{5,6},{6,5},{7,8},{8,7},{9,10},{10,9},{11,... | collective-permute-start | bytes 2752520 | tf_op jit(solution)/shard_map/ppermute | solution.py:21
  143.1 17.2 %collective-permute-done.14 = f32[128,1024]{1,0:T(8,128)S(1)} collective-permute-done((f32[128,1024]{1,0:T(8,128)S(1)}, f32[128,1024]{1,0:T(8,128)S(1)}, u32[]{:S(2)}, u32[]{:S(2)}) %collective-permute-start.14) | collective-permute-done | bytes 524320 | tf_op jit(solution)/shard_map/ppermute | solution.py:21
  160.5 6.8 %collective-permute-done.16 = f32[160,1024]{1,0:T(8,128)S(1)} collective-permute-done((f32[160,1024]{1,0:T(8,128)S(1)}, f32[160,1024]{1,0:T(8,128)S(1)}, u32[]{:S(2)}, u32[]{:S(2)}) %collective-permute-start.16) | collective-permute-done | bytes 655392 | tf_op jit(solution)/shard_map/ppermute | solution.py:21
  167.6 16.6 %collective-permute-done.18 = f32[224,1024]{1,0:T(8,128)S(1)} collective-permute-done((f32[224,1024]{1,0:T(8,128)S(1)}, f32[224,1024]{1,0:T(8,128)S(1)}, u32[]{:S(2)}, u32[]{:S(2)}) %collective-permute-start.18) | collective-permute-done | bytes 917536 | tf_op jit(solution)/shard_map/ppermute | solution.py:21
  185.5 1.1 multiply_reduce_fusion.1
  189.7 4.4 %collective-permute-start.22 = (f32[160,1024]{1,0:T(8,128)S(1)}, f32[160,1024]{1,0:T(8,128)S(1)}, u32[]{:S(2)}, u32[]{:S(2)}) collective-permute-start(f32[160,1024]{1,0:T(8,128)S(1)} %get-tuple-element.169), channel_id=1, source_target_pairs={{1,2},{2,1},{3,4},{4,3},{5,6},{6,5},{7,8},{8,7},{9,10},{10,9},{11,... | collective-permute-start | bytes 1966088 | tf_op jit(solution)/shard_map/ppermute | solution.py:21
  194.2 2.2 collective-permute-start.20
  198.7 12.7 %collective-permute-done.22 = f32[160,1024]{1,0:T(8,128)S(1)} collective-permute-done((f32[160,1024]{1,0:T(8,128)S(1)}, f32[160,1024]{1,0:T(8,128)S(1)}, u32[]{:S(2)}, u32[]{:S(2)}) %collective-permute-start.22) | collective-permute-done | bytes 655392 | tf_op jit(solution)/shard_map/ppermute | solution.py:21
  211.7 10.3 %collective-permute-done.20 = f32[224,1024]{1,0:T(8,128)S(1)} collective-permute-done((f32[224,1024]{1,0:T(8,128)S(1)}, f32[224,1024]{1,0:T(8,128)S(1)}, u32[]{:S(2)}, u32[]{:S(2)}) %collective-permute-start.20) | collective-permute-done | bytes 917536 | tf_op jit(solution)/shard_map/ppermute | solution.py:21
  227.0 2.1 fusion.60
  (158 shorter events, 37.8 us)
Async XLA Ops:
  0.6 1.9 copy-start
  0.6 1.9 copy-start.1
  4.0 6.0 %copy-start.2 = (f32[1,512,1024]{2,1,0:T(8,128)S(1)}, f32[1,512,1024]{2,1,0:T(8,128)}, u32[]{:S(2)}) copy-start(f32[1,512,1024]{2,1,0:T(8,128)} %param.7) | copy-start | bytes 6291460
  4.0 5.9 %copy-start.4 = (f32[1,512,1024]{2,1,0:T(8,128)S(1)}, f32[1,512,1024]{2,1,0:T(8,128)}, u32[]{:S(2)}) copy-start(f32[1,512,1024]{2,1,0:T(8,128)} %param.6) | copy-start | bytes 6291460
  5.2 20.5 %collective-permute-start = (f32[128,1024]{1,0:T(8,128)}, f32[128,1024]{1,0:T(8,128)}, u32[]{:S(2)}, u32[]{:S(2)}) collective-permute-start(f32[128,1024]{1,0:T(8,128)} %get-tuple-element.92), channel_id=1, source_target_pairs={{1,2},{2,1},{3,4},{4,3},{5,6},{6,5},{7,8},{8,7},{9,10},{10,9},{11,... | collective-permute-start | bytes 1572872 | tf_op jit(solution)/shard_map/ppermute | solution.py:21
  9.9 16.0 %collective-permute-start.1 = (f32[128,1024]{1,0:T(8,128)S(1)}, f32[128,1024]{1,0:T(8,128)}, u32[]{:S(2)}, u32[]{:S(2)}) collective-permute-start(f32[128,1024]{1,0:T(8,128)S(1)} %broadcast_select_fusion.23), channel_id=1, source_target_pairs={{0,1},{1,0},{2,3},{3,2},{4,5},{5,4},{6,7},{7,6},{8,9},{9,8},{10,11... | collective-permute-start | bytes 1572872 | tf_op jit(solution)/shard_map/ppermute | solution.py:21
  18.7 33.8 %collective-permute-start.4 = (f32[160,1024]{1,0:T(8,128)}, f32[160,1024]{1,0:T(8,128)}, u32[]{:S(2)}, u32[]{:S(2)}) collective-permute-start(f32[160,1024]{1,0:T(8,128)} %get-tuple-element.108), channel_id=1, source_target_pairs={{1,2},{2,1},{3,4},{4,3},{5,6},{6,5},{7,8},{8,7},{9,10},{10,9},{11,... | collective-permute-start | bytes 1966088 | tf_op jit(solution)/shard_map/ppermute | solution.py:21
  22.1 30.3 %collective-permute-start.5 = (f32[160,1024]{1,0:T(8,128)}, f32[160,1024]{1,0:T(8,128)}, u32[]{:S(2)}, u32[]{:S(2)}) collective-permute-start(f32[160,1024]{1,0:T(8,128)} %broadcast_select_fusion.15), channel_id=1, source_target_pairs={{0,1},{1,0},{2,3},{3,2},{4,5},{5,4},{6,7},{7,6},{8,9},{9,8},{10,11... | collective-permute-start | bytes 1966088 | tf_op jit(solution)/shard_map/ppermute | solution.py:21
  22.2 40.0 %collective-permute-start.6 = (f32[224,1024]{1,0:T(8,128)}, f32[224,1024]{1,0:T(8,128)S(1)}, u32[]{:S(2)}, u32[]{:S(2)}) collective-permute-start(f32[224,1024]{1,0:T(8,128)} %get-tuple-element.110), channel_id=1, source_target_pairs={{1,2},{2,1},{3,4},{4,3},{5,6},{6,5},{7,8},{8,7},{9,10},{10,9},{11,... | collective-permute-start | bytes 2752520 | tf_op jit(solution)/shard_map/ppermute | solution.py:21
  25.7 36.5 %collective-permute-start.7 = (f32[224,1024]{1,0:T(8,128)}, f32[224,1024]{1,0:T(8,128)S(1)}, u32[]{:S(2)}, u32[]{:S(2)}) collective-permute-start(f32[224,1024]{1,0:T(8,128)} %broadcast_select_fusion.7), channel_id=1, source_target_pairs={{0,1},{1,0},{2,3},{3,2},{4,5},{5,4},{6,7},{7,6},{8,9},{9,8},{10,11... | collective-permute-start | bytes 2752520 | tf_op jit(solution)/shard_map/ppermute | solution.py:21
  29.1 23.4 %copy-start.3 = (f32[1,512,1024]{2,1,0:T(8,128)S(1)}, f32[1,512,1024]{2,1,0:T(8,128)}, u32[]{:S(2)}) copy-start(f32[1,512,1024]{2,1,0:T(8,128)} %param.7) | copy-start | bytes 6291460
  29.1 23.4 %copy-start.5 = (f32[1,512,1024]{2,1,0:T(8,128)S(1)}, f32[1,512,1024]{2,1,0:T(8,128)}, u32[]{:S(2)}) copy-start(f32[1,512,1024]{2,1,0:T(8,128)} %param.6) | copy-start | bytes 6291460
  29.5 43.8 %collective-permute-start.2 = (f32[128,1024]{1,0:T(8,128)S(1)}, f32[128,1024]{1,0:T(8,128)S(1)}, u32[]{:S(2)}, u32[]{:S(2)}) collective-permute-start(f32[128,1024]{1,0:T(8,128)S(1)} %get-tuple-element.106), channel_id=1, source_target_pairs={{1,2},{2,1},{3,4},{4,3},{5,6},{6,5},{7,8},{8,7},{9,10},{10,9},{11,... | collective-permute-start | bytes 1572872 | tf_op jit(solution)/shard_map/ppermute | solution.py:21
  52.4 21.0 %collective-permute-start.3 = (f32[128,1024]{1,0:T(8,128)S(1)}, f32[128,1024]{1,0:T(8,128)S(1)}, u32[]{:S(2)}, u32[]{:S(2)}) collective-permute-start(f32[128,1024]{1,0:T(8,128)S(1)} %broadcast_select_fusion.21), channel_id=1, source_target_pairs={{0,1},{1,0},{2,3},{3,2},{4,5},{5,4},{6,7},{7,6},{8,9},{9,8},{10,11... | collective-permute-start | bytes 1572872 | tf_op jit(solution)/shard_map/ppermute | solution.py:21
  75.6 27.4 %collective-permute-start.8 = (f32[128,1024]{1,0:T(8,128)S(1)}, f32[128,1024]{1,0:T(8,128)S(1)}, u32[]{:S(2)}, u32[]{:S(2)}) collective-permute-start(f32[128,1024]{1,0:T(8,128)S(1)} %get-tuple-element.124), channel_id=1, source_target_pairs={{1,2},{2,1},{3,4},{4,3},{5,6},{6,5},{7,8},{8,7},{9,10},{10,9},{11,... | collective-permute-start | bytes 1572872 | tf_op jit(solution)/shard_map/ppermute | solution.py:21
  80.0 23.0 %collective-permute-start.9 = (f32[128,1024]{1,0:T(8,128)S(1)}, f32[128,1024]{1,0:T(8,128)S(1)}, u32[]{:S(2)}, u32[]{:S(2)}) collective-permute-start(f32[128,1024]{1,0:T(8,128)S(1)} %broadcast_select_fusion.19), channel_id=1, source_target_pairs={{0,1},{1,0},{2,3},{3,2},{4,5},{5,4},{6,7},{7,6},{8,9},{9,8},{10,11... | collective-permute-start | bytes 1572872 | tf_op jit(solution)/shard_map/ppermute | solution.py:21
  80.1 29.9 %collective-permute-start.10 = (f32[160,1024]{1,0:T(8,128)S(1)}, f32[160,1024]{1,0:T(8,128)S(1)}, u32[]{:S(2)}, u32[]{:S(2)}) collective-permute-start(f32[160,1024]{1,0:T(8,128)S(1)} %get-tuple-element.126), channel_id=1, source_target_pairs={{1,2},{2,1},{3,4},{4,3},{5,6},{6,5},{7,8},{8,7},{9,10},{10,9},{11,... | collective-permute-start | bytes 1966088 | tf_op jit(solution)/shard_map/ppermute | solution.py:21
  82.0 28.0 %collective-permute-start.11 = (f32[160,1024]{1,0:T(8,128)S(1)}, f32[160,1024]{1,0:T(8,128)S(1)}, u32[]{:S(2)}, u32[]{:S(2)}) collective-permute-start(f32[160,1024]{1,0:T(8,128)S(1)} %broadcast_select_fusion.13), channel_id=1, source_target_pairs={{0,1},{1,0},{2,3},{3,2},{4,5},{5,4},{6,7},{7,6},{8,9},{9,8},{10,11... | collective-permute-start | bytes 1966088 | tf_op jit(solution)/shard_map/ppermute | solution.py:21
  82.1 43.3 %collective-permute-start.12 = (f32[224,1024]{1,0:T(8,128)S(1)}, f32[224,1024]{1,0:T(8,128)S(1)}, u32[]{:S(2)}, u32[]{:S(2)}) collective-permute-start(f32[224,1024]{1,0:T(8,128)S(1)} %get-tuple-element.128), channel_id=1, source_target_pairs={{1,2},{2,1},{3,4},{4,3},{5,6},{6,5},{7,8},{8,7},{9,10},{10,9},{11,... | collective-permute-start | bytes 2752520 | tf_op jit(solution)/shard_map/ppermute | solution.py:21
  103.0 22.5 %collective-permute-start.13 = (f32[224,1024]{1,0:T(8,128)S(1)}, f32[224,1024]{1,0:T(8,128)S(1)}, u32[]{:S(2)}, u32[]{:S(2)}) collective-permute-start(f32[224,1024]{1,0:T(8,128)S(1)} %broadcast_select_fusion.5), channel_id=1, source_target_pairs={{0,1},{1,0},{2,3},{3,2},{4,5},{5,4},{6,7},{7,6},{8,9},{9,8},{10,11... | collective-permute-start | bytes 2752520 | tf_op jit(solution)/shard_map/ppermute | solution.py:21
  132.9 27.4 %collective-permute-start.14 = (f32[128,1024]{1,0:T(8,128)S(1)}, f32[128,1024]{1,0:T(8,128)S(1)}, u32[]{:S(2)}, u32[]{:S(2)}) collective-permute-start(f32[128,1024]{1,0:T(8,128)S(1)} %get-tuple-element.142), channel_id=1, source_target_pairs={{1,2},{2,1},{3,4},{4,3},{5,6},{6,5},{7,8},{8,7},{9,10},{10,9},{11,... | collective-permute-start | bytes 1572872 | tf_op jit(solution)/shard_map/ppermute | solution.py:21
  137.3 23.0 %collective-permute-start.15 = (f32[128,1024]{1,0:T(8,128)S(1)}, f32[128,1024]{1,0:T(8,128)S(1)}, u32[]{:S(2)}, u32[]{:S(2)}) collective-permute-start(f32[128,1024]{1,0:T(8,128)S(1)} %broadcast_select_fusion.17), channel_id=1, source_target_pairs={{0,1},{1,0},{2,3},{3,2},{4,5},{5,4},{6,7},{7,6},{8,9},{9,8},{10,11... | collective-permute-start | bytes 1572872 | tf_op jit(solution)/shard_map/ppermute | solution.py:21
  137.4 29.9 %collective-permute-start.16 = (f32[160,1024]{1,0:T(8,128)S(1)}, f32[160,1024]{1,0:T(8,128)S(1)}, u32[]{:S(2)}, u32[]{:S(2)}) collective-permute-start(f32[160,1024]{1,0:T(8,128)S(1)} %get-tuple-element.144), channel_id=1, source_target_pairs={{1,2},{2,1},{3,4},{4,3},{5,6},{6,5},{7,8},{8,7},{9,10},{10,9},{11,... | collective-permute-start | bytes 1966088 | tf_op jit(solution)/shard_map/ppermute | solution.py:21
  139.3 28.0 %collective-permute-start.17 = (f32[160,1024]{1,0:T(8,128)S(1)}, f32[160,1024]{1,0:T(8,128)S(1)}, u32[]{:S(2)}, u32[]{:S(2)}) collective-permute-start(f32[160,1024]{1,0:T(8,128)S(1)} %broadcast_select_fusion.11), channel_id=1, source_target_pairs={{0,1},{1,0},{2,3},{3,2},{4,5},{5,4},{6,7},{7,6},{8,9},{9,8},{10,11... | collective-permute-start | bytes 1966088 | tf_op jit(solution)/shard_map/ppermute | solution.py:21
  139.4 44.7 %collective-permute-start.18 = (f32[224,1024]{1,0:T(8,128)S(1)}, f32[224,1024]{1,0:T(8,128)S(1)}, u32[]{:S(2)}, u32[]{:S(2)}) collective-permute-start(f32[224,1024]{1,0:T(8,128)S(1)} %get-tuple-element.146), channel_id=1, source_target_pairs={{1,2},{2,1},{3,4},{4,3},{5,6},{6,5},{7,8},{8,7},{9,10},{10,9},{11,... | collective-permute-start | bytes 2752520 | tf_op jit(solution)/shard_map/ppermute | solution.py:21
  160.3 23.9 %collective-permute-start.19 = (f32[224,1024]{1,0:T(8,128)S(1)}, f32[224,1024]{1,0:T(8,128)S(1)}, u32[]{:S(2)}, u32[]{:S(2)}) collective-permute-start(f32[224,1024]{1,0:T(8,128)S(1)} %broadcast_select_fusion.3), channel_id=1, source_target_pairs={{0,1},{1,0},{2,3},{3,2},{4,5},{5,4},{6,7},{7,6},{8,9},{9,8},{10,11... | collective-permute-start | bytes 2752520 | tf_op jit(solution)/shard_map/ppermute | solution.py:21
  189.7 21.7 %collective-permute-start.22 = (f32[160,1024]{1,0:T(8,128)S(1)}, f32[160,1024]{1,0:T(8,128)S(1)}, u32[]{:S(2)}, u32[]{:S(2)}) collective-permute-start(f32[160,1024]{1,0:T(8,128)S(1)} %get-tuple-element.169), channel_id=1, source_target_pairs={{1,2},{2,1},{3,4},{4,3},{5,6},{6,5},{7,8},{8,7},{9,10},{10,9},{11,... | collective-permute-start | bytes 1966088 | tf_op jit(solution)/shard_map/ppermute | solution.py:21
  194.1 17.3 %collective-permute-start.23 = (f32[160,1024]{1,0:T(8,128)S(1)}, f32[160,1024]{1,0:T(8,128)S(1)}, u32[]{:S(2)}, u32[]{:S(2)}) collective-permute-start(f32[160,1024]{1,0:T(8,128)S(1)} %broadcast_select_fusion.9), channel_id=1, source_target_pairs={{0,1},{1,0},{2,3},{3,2},{4,5},{5,4},{6,7},{7,6},{8,9},{9,8},{10,11... | collective-permute-start | bytes 1966088 | tf_op jit(solution)/shard_map/ppermute | solution.py:21
  194.2 27.8 %collective-permute-start.20 = (f32[224,1024]{1,0:T(8,128)S(1)}, f32[224,1024]{1,0:T(8,128)S(1)}, u32[]{:S(2)}, u32[]{:S(2)}) collective-permute-start(f32[224,1024]{1,0:T(8,128)S(1)} %get-tuple-element.161), channel_id=1, source_target_pairs={{1,2},{2,1},{3,4},{4,3},{5,6},{6,5},{7,8},{8,7},{9,10},{10,9},{11,... | collective-permute-start | bytes 2752520 | tf_op jit(solution)/shard_map/ppermute | solution.py:21
  196.3 25.7 %collective-permute-start.21 = (f32[224,1024]{1,0:T(8,128)S(1)}, f32[224,1024]{1,0:T(8,128)S(1)}, u32[]{:S(2)}, u32[]{:S(2)}) collective-permute-start(f32[224,1024]{1,0:T(8,128)S(1)} %broadcast_select_fusion.1), channel_id=1, source_target_pairs={{0,1},{1,0},{2,3},{3,2},{4,5},{5,4},{6,7},{7,6},{8,9},{9,8},{10,11... | collective-permute-start | bytes 2752520 | tf_op jit(solution)/shard_map/ppermute | solution.py:21
